TPU v7x, 32 devices: a whole 2x2x4 slice. The times are simulated.
32 devices in a mesh: groups: 2 (over y), freq: 16 (over z, x, core).
Axes of the slice: x: 2, y: 2, z: 4, core: 2. Of those that a mesh axis runs over, the one named last changes fastest.
Arguments:
- primary_one: bfloat16 [1024, 512, 512], P(('groups', 'freq')), parts along dimension 0, may hold values from -6 to 6
- primary_two: bfloat16 [1024, 512, 512], P(('groups', 'freq')), parts along dimension 0, may hold values from -6 to 6
- primary_three: bfloat16 [1024, 512, 512], P(('groups', 'freq')), parts along dimension 0, may hold values from -6 to 6
- window_start: int32 [3, 1024, 512], P(None, ('groups', 'freq')), parts along dimension 1, may hold values from 0 to 255
- window_end: int32 [3, 1024, 512], P(None, ('groups', 'freq')), parts along dimension 1, may hold values from 257 to 512
Outputs:
- predicted: bfloat16 [1024, 512, 512], P(('groups', 'freq')), parts along dimension 0
There are 2 independent parts, one for each index of `groups`. A program takes and returns all parts, laid end to end along the dimension named above; each array names one. Nothing has to cross between parts.
Inputs may be any that keep to these rules, and one draw needn't show every extreme that they name: window_start of a trace is below its window_end.
All inputs are finite; a program needn't handle non-finite values.
Results may differ from a plain program's by a relative error of at most 0.0089.
Values may be sent and summed in bfloat16 or wider, within the bound.
A program may use at most 128 MiB of HBM per device.

v0:
```python
import functools

import jax
import jax.numpy as jnp
from jax import lax
from jax.experimental import pallas as pl
from jax.experimental.pallas import tpu as pltpu
from jax.sharding import PartitionSpec as P

F_DEV = 1
GROUP = 16
LANES = 128


def make_table(count, samples):
    waves = jnp.arange(1, count + 1, dtype=jnp.int32)[:, None]
    times = jnp.arange(samples, dtype=jnp.int32)[None, :]
    phase = waves * times % samples
    angle = 2.0 * jnp.pi / samples * phase.astype(jnp.float32)
    both = jnp.stack([jnp.cos(angle), -jnp.sin(angle)], axis=1)
    return both.reshape(2 * count, samples).astype(jnp.bfloat16)


def exchange_kernel(
    n, sub, one_ref, two_ref, three_ref, start_ref, end_ref, table_ref, out_ref,
    buf, scr, stage, r1, r2, r3, gw, mbuf,
    load_sem, send_sem, r1_sem, r23_sem, out_sem,
):
    me = lax.axis_index("freq")
    sources, receivers, samples = one_ref.shape
    half = n // 2
    side = me // half
    n_sub = GROUP // sub
    total = sources // sub

    def peer_far(q):
        return (1 - side) * half + lax.rem(me + q, half)

    def peer_near(q):
        return side * half + lax.rem(me + q, half)

    barrier = pltpu.get_barrier_semaphore()

    @pl.loop(1, n)
    def _(q):
        pl.semaphore_signal(
            barrier, inc=1, device_id={"freq": lax.rem(me + q, n)},
            device_id_type=pl.DeviceIdType.MESH,
        )

    sets = ((two_ref, 1, r2), (three_ref, 2, r3), (one_ref, 0, r1))

    def load(ref, i, slot):
        return pltpu.make_async_copy(
            ref.at[pl.ds(i * sub, sub)], buf.at[slot], load_sem.at[slot]
        )

    load(sets[0][0], 0, 0).start()
    scale_t = 1.0 / (samples ** 0.5)

    for k, (ref, which, landing) in enumerate(sets):
        if k < 2:
            arrive = r23_sem.at[k]
        else:
            arrive = r1_sem.at[me]

        @pl.loop(0, sources // GROUP)
        def _(g):
            @pl.loop(0, n_sub)
            def _(j):
                i = g * n_sub + j
                slot = lax.rem(i, 2)

                @pl.when(i + 1 < total)
                def _():
                    load(ref, i + 1, 1 - slot).start()

                if k < 2:
                    @pl.when(i + 1 == total)
                    def _():
                        load(sets[k + 1][0], 0, 0).start()

                load(ref, i, slot).wait()
                for s in range(sub):
                    row = i * sub + s
                    packed = (
                        start_ref[which, pl.ds(row, 1), :] * 4096
                        + end_ref[which, pl.ds(row, 1), :]
                    )
                    packed = jnp.broadcast_to(packed, (LANES, receivers)).T
                    first = packed >> 12
                    last = packed & 4095
                    lane = lax.broadcasted_iota(jnp.int32, (receivers, LANES), 1)
                    pieces = []
                    for c in range(samples // LANES):
                        x = buf[slot, s, :, c * LANES:(c + 1) * LANES]
                        t = lane + c * LANES
                        keep = (t >= first) & (t < last)
                        pieces.append(jnp.where(keep, x, jnp.zeros_like(x)))
                    windowed = jnp.concatenate(pieces, axis=1)
                    spec = lax.dot_general(
                        table_ref[...], windowed, (((1,), (1,)), ((), ())),
                        preferred_element_type=jnp.float32,
                    )
                    scr[j * sub + s] = spec * scale_t

            at = pl.ds(pl.multiple_of(g * GROUP, GROUP), GROUP)
            for w in range(2 * n):
                stage[k, w // 2, w % 2, at, :] = scr[:, w, :].astype(jnp.bfloat16)

            if k == 0:
                @pl.when(g == 0)
                def _():
                    pl.semaphore_wait(barrier, n - 1)

                send_rows(k, g * GROUP, GROUP, landing, arrive, me, n, sources,
                          half, peer_far, peer_near, stage, send_sem)

        if k > 0:
            send_rows(k, 0, sources, landing, arrive, me, n, sources,
                      half, peer_far, peer_near, stage, send_sem)

    def drain(ref, sem):
        pltpu.make_async_copy(ref, ref, sem).wait()

    drain(r2, r23_sem.at[0])
    drain(r3, r23_sem.at[1])
    scale_g = 1.0 / ((n * sources) ** 0.5)
    scale_m = 1.0 / (receivers ** 0.5)
    width = 256

    @pl.loop(0, receivers // width)
    def _(b):
        cols = pl.ds(pl.multiple_of(b * width, width), width)
        ct = r2[0, :, cols].T
        dt = r2[1, :, cols].T
        e = r3[0]
        f = r3[1]
        dot = functools.partial(jnp.dot, preferred_element_type=jnp.float32)
        gw[cols, :receivers] = ((dot(ct, e) + dot(dt, f)) * scale_g).astype(jnp.bfloat16)
        gw[cols, receivers:] = ((dot(ct, f) - dot(dt, e)) * scale_g).astype(jnp.bfloat16)

    @pl.loop(0, n)
    def _(step):
        place = lax.rem(me + n - step, half)
        p = jnp.where(step < half, side, 1 - side) * half + place
        rows = pl.ds(pl.multiple_of(p * sources, sources), sources)
        drain(r1.at[:, rows, :], r1_sem.at[p])
        both = jnp.concatenate([r1[0, rows, :], r1[1, rows, :]], axis=0)
        prod = jnp.dot(both, gw[...], preferred_element_type=jnp.float32)
        re = prod[:sources, :receivers] - prod[sources:, receivers:]
        im = prod[:sources, receivers:] + prod[sources:, :receivers]
        mbuf[0, rows, :] = (re * scale_m).astype(jnp.bfloat16)
        mbuf[1, rows, :] = (im * scale_m).astype(jnp.bfloat16)
        src = mbuf.at[:, rows, :]

        @pl.when(p != me)
        def _():
            pltpu.make_async_remote_copy(
                src_ref=src, dst_ref=out_ref.at[me],
                send_sem=send_sem.at[3], recv_sem=out_sem,
                device_id={"freq": p}, device_id_type=pl.DeviceIdType.MESH,
            ).start()

        @pl.when(p == me)
        def _():
            pltpu.make_async_copy(src, out_ref.at[me], out_sem).start()

    drain(out_ref, out_sem)
    for k in range(3):
        drain(stage.at[k, pl.ds(0, n - 1)], send_sem.at[k])
    drain(out_ref.at[pl.ds(0, n - 1)], send_sem.at[3])


def send_rows(k, base, count, landing, arrive, me, n, sources, half,
              peer_far, peer_near, stage, send_sem):
    if not isinstance(base, int):
        base = pl.multiple_of(base, GROUP)
    here = pl.ds(base, count)
    there = pl.ds(pl.multiple_of(me * sources + base, GROUP), count)

    def send(p):
        pltpu.make_async_remote_copy(
            src_ref=stage.at[k, p, :, here, :], dst_ref=landing.at[:, there, :],
            send_sem=send_sem.at[k], recv_sem=arrive,
            device_id={"freq": p}, device_id_type=pl.DeviceIdType.MESH,
        ).start()

    def far():
        @pl.loop(0, half)
        def _(q):
            send(peer_far(q))

    def near():
        pltpu.make_async_copy(
            stage.at[k, me, :, here, :], landing.at[:, there, :], arrive
        ).start()

        @pl.loop(1, half)
        def _(q):
            send(peer_near(q))

    if k == 2:
        near()
        far()
    else:
        far()
        near()


def inverse_kernel(piece_ref, table_ref, out_ref, scr):
    count = piece_ref.shape[0]
    step = pl.program_id(0)
    sub = out_ref.shape[0]
    per = GROUP // sub

    @pl.when(lax.rem(step, per) == 0)
    def _():
        at = pl.ds(pl.multiple_of(step // per * GROUP, GROUP), GROUP)
        for w in range(2 * count):
            scr[:, w, :] = piece_ref[w // 2, w % 2, at, :].astype(jnp.float32)

    scale = 1.0 / (count ** 0.5)
    for s in range(sub):
        row = lax.rem(step, per) * sub + s
        timed = lax.dot_general(
            scr[row].astype(jnp.bfloat16), table_ref[...],
            (((0,), (0,)), ((), ())), preferred_element_type=jnp.float32,
        )
        out_ref[s] = (timed * scale).astype(jnp.bfloat16)


def spectrum(traces, start, finish, table, count):
    sources, receivers, samples = traces.shape
    times = jnp.arange(samples, dtype=jnp.int32)
    inside = (times >= start[:, :, None]) & (times < finish[:, :, None])
    windowed = jnp.where(inside, traces, jnp.zeros_like(traces))
    flat = windowed.reshape(sources * receivers, samples)
    spec = lax.dot_general(
        table, flat, (((1,), (1,)), ((), ())), preferred_element_type=jnp.float32
    )
    spec = spec * (1.0 / jnp.sqrt(jnp.float32(samples)))
    return spec.astype(jnp.bfloat16).reshape(count, 2, sources, receivers)


def correlate(first, second):
    swapped = jnp.stack([first[:, 1], -first[:, 0]], axis=1)
    left = jnp.stack([first, swapped], axis=1)
    cross = jnp.einsum("fkcsr,fcur->fksu", left, second, preferred_element_type=jnp.float32)
    cross = cross * (1.0 / jnp.sqrt(jnp.float32(first.shape[3])))
    return cross.astype(jnp.bfloat16)


def convolve(cross, third):
    right = jnp.stack(
        [
            jnp.stack([third[:, 0], -third[:, 1]], axis=1),
            jnp.stack([third[:, 1], third[:, 0]], axis=1),
        ],
        axis=1,
    )
    multiple = jnp.einsum("fcsu,fkcur->fksr", cross, right, preferred_element_type=jnp.float32)
    multiple = multiple * (1.0 / jnp.sqrt(jnp.float32(third.shape[2])))
    return multiple.astype(jnp.bfloat16)


def plain_on_device(primary_one, primary_two, primary_three, window_start, window_end):
    samples = primary_one.shape[2]
    count = F_DEV * lax.axis_size("freq")
    table = make_table(count, samples)
    spec_one = spectrum(primary_one, window_start[0], window_end[0], table, count)
    spec_two = spectrum(primary_two, window_start[1], window_end[1], table, count)
    spec_three = spectrum(primary_three, window_start[2], window_end[2], table, count)
    first, second, third = (
        lax.all_to_all(spec_one, "freq", split_axis=0, concat_axis=2, tiled=True),
        lax.all_to_all(spec_two, "freq", split_axis=0, concat_axis=2, tiled=True),
        lax.all_to_all(spec_three, "freq", split_axis=0, concat_axis=2, tiled=True),
    )
    cross = correlate(first, second)
    multiple = convolve(cross, third)
    piece = lax.all_to_all(multiple, "freq", split_axis=2, concat_axis=0, tiled=True)
    waves, parts, sources, receivers = piece.shape
    flat = piece.reshape(waves * parts, sources * receivers)
    timed = lax.dot_general(
        flat, table, (((0,), (0,)), ((), ())), preferred_element_type=jnp.float32
    )
    timed = timed * (1.0 / jnp.sqrt(jnp.float32(count)))
    return timed.astype(jnp.bfloat16).reshape(sources, receivers, samples)


def on_device(primary_one, primary_two, primary_three, window_start, window_end):
    sources, receivers, samples = primary_one.shape
    n = lax.axis_size("freq")
    if sources % GROUP or n % 2 or receivers % 256 or samples % LANES:
        return plain_on_device(
            primary_one, primary_two, primary_three, window_start, window_end
        )
    count = F_DEV * n
    table = make_table(count, samples)
    sub = max(1, min(GROUP // 2, (2 << 20) // (receivers * samples * 2)))
    bf = jnp.bfloat16
    whole = n * sources
    vmem = pl.BlockSpec(memory_space=pltpu.VMEM)
    hbm = pl.BlockSpec(memory_space=pl.ANY)
    piece = pl.pallas_call(
        functools.partial(exchange_kernel, n, sub),
        out_shape=jax.ShapeDtypeStruct((n, 2, sources, receivers), bf),
        in_specs=[hbm, hbm, hbm, vmem, vmem, vmem],
        out_specs=vmem,
        scratch_shapes=[
            pltpu.VMEM((2, sub, receivers, samples), bf),
            pltpu.VMEM((GROUP, 2 * count, receivers), jnp.float32),
            pltpu.VMEM((3, n, 2, sources, receivers), bf),
            pltpu.VMEM((2, whole, receivers), bf),
            pltpu.VMEM((2, whole, receivers), bf),
            pltpu.VMEM((2, whole, receivers), bf),
            pltpu.VMEM((receivers, 2 * receivers), bf),
            pltpu.VMEM((2, whole, receivers), bf),
            pltpu.SemaphoreType.DMA((2,)),
            pltpu.SemaphoreType.DMA((4,)),
            pltpu.SemaphoreType.DMA((n,)),
            pltpu.SemaphoreType.DMA((2,)),
            pltpu.SemaphoreType.DMA,
        ],
        compiler_params=pltpu.CompilerParams(
            collective_id=0, has_side_effects=True, vmem_limit_bytes=67000000,
        ),
        name="exchange",
    )(primary_one, primary_two, primary_three, window_start, window_end, table)
    return pl.pallas_call(
        inverse_kernel,
        out_shape=jax.ShapeDtypeStruct(primary_one.shape, bf),
        grid=(sources // sub,),
        in_specs=[vmem, vmem],
        out_specs=pl.BlockSpec((sub, receivers, samples), lambda i: (i, 0, 0)),
        scratch_shapes=[pltpu.VMEM((GROUP, 2 * count, receivers), jnp.float32)],
        name="inverse",
    )(piece, table)


def solution(mesh):
    return jax.shard_map(
        on_device,
        mesh=mesh,
        in_specs=(
            P(("groups", "freq"), None, None),
            P(("groups", "freq"), None, None),
            P(("groups", "freq"), None, None),
            P(None, ("groups", "freq"), None),
            P(None, ("groups", "freq"), None),
        ),
        out_specs=P(("groups", "freq"), None, None),
        check_vma=False,
    )
```

profile of v0, /device:TPU:1, one launch (start us, length us, event | category | flops | bytes accessed | tf_op | source)
XLA Modules:
  0.0 116.2 jit_solution(4624027678285258838)
XLA Ops:
  0.0 0.2 cosine_convert_fusion
  0.3 0.6 convert_element_type.20.table_ref
  0.9 104.5 %exchange.1.piece_ref = bf16[16,2,32,512]{3,2,1,0:T(8,128)(2,1)} custom-call(bf16[32,512,512]{2,1,0:T(8,128)(2,1)} %one_ref.1, bf16[32,512,512]{2,1,0:T(8,128)(2,1)} %two_ref.1, bf16[32,512,512]{2,1,0:T(8,128)(2,1)} %three_ref.1, s32[3,32,512]{2,1,0:T(8,128)} %start_ref.1, s32[3,32,512]{2,1,0:T(8,128)} %end_ref.1, bf16[32,512]{1,0:T(8,128)(2,1)} %convert_element_type.20.table_ref), custom_call_target="tpu_custom_call" | custom-call | tf_op jit(solution)/shard_map/exchange/pallas_call | solution.py:305
  105.4 10.8 %inverse.1 = bf16[32,512,512]{2,1,0:T(8,128)(2,1)} custom-call(bf16[16,2,32,512]{3,2,1,0:T(8,128)(2,1)} %exchange.1.piece_ref, bf16[32,512]{1,0:T(8,128)(2,1)} %convert_element_type.20.table_ref), custom_call_target="tpu_custom_call" | custom-call | tf_op jit(solution)/shard_map/inverse/pallas_call | solution.py:330
  (3 shorter events, 0.0 us)
where the time goes:
time: 117 us; the launch traced here: 116 us
  Pallas kernels  115 us (98%)
    pallas_call x1, Pallas kernels, on_device(): pl.pallas_call(functools.partial(exchange_kernel, n, sub), out_shape=jax....  105 us
    pallas_call x1, Pallas kernels, on_device(): pl.pallas_call(inverse_kernel, out_shape=jax.ShapeDtypeStruct(primary_one...  10.8 us

commit v1 on v0

v1 whole, which is shorter than its diff:
```python
import functools
import math

import jax
import jax.numpy as jnp
import numpy as np
from jax import lax
from jax.experimental import pallas as pl
from jax.experimental.pallas import tpu as pltpu
from jax.sharding import PartitionSpec as P

F_DEV = 1
CHUNK = 8
PAIR = 2 * CHUNK
SUB = 2
SLOTS = 4
LANES = 128


def make_table(count, samples):
    waves = jnp.arange(1, count + 1, dtype=jnp.int32)[:, None]
    times = jnp.arange(samples, dtype=jnp.int32)[None, :]
    phase = waves * times % samples
    angle = 2.0 * jnp.pi / samples * phase.astype(jnp.float32)
    both = jnp.stack([jnp.cos(angle), -jnp.sin(angle)], axis=1)
    return both.reshape(2 * count, samples).astype(jnp.bfloat16)


def host_table(count, samples):
    waves = np.arange(1, count + 1, dtype=np.int64)[:, None]
    times = np.arange(samples, dtype=np.int64)[None, :]
    phase = waves * times % samples
    angle = np.float32(2.0 * np.pi / samples) * phase.astype(np.float32)
    both = np.stack([np.cos(angle), -np.sin(angle)], axis=1)
    return jnp.asarray(both.reshape(2 * count, samples).astype(jnp.bfloat16))


def drain(ref, sem):
    pltpu.make_async_copy(ref, ref, sem).wait()


def exchange_kernel(
    n, one_ref, two_ref, three_ref, start_hbm, end_hbm, table_hbm,
    early_ref, last_ref, wide_ref,
    start_ref, end_ref, table_ref, buf, scr, stage, r1, r2, r3, r3s, gw, mbuf, piece, turned,
    load_sem, small_sem, send_sem, r1_sem, r23_sem, out_sem,
):
    me = lax.axis_index("freq")
    sources, receivers, samples = one_ref.shape
    half = n // 2
    side = me // half
    chunks = sources // CHUNK
    total = sources // SUB
    waves = 2 * n
    middle = samples // 2
    bf = jnp.bfloat16
    f32 = jnp.float32

    def peer_far(q):
        return (1 - side) * half + lax.rem(me + q, half)

    def peer_near(q):
        return side * half + lax.rem(me + q, half)

    barrier = pltpu.get_barrier_semaphore()

    @pl.loop(1, n)
    def _(q):
        pl.semaphore_signal(
            barrier, inc=1, device_id={"freq": lax.rem(me + q, n)},
            device_id_type=pl.DeviceIdType.MESH,
        )

    sets = ((two_ref, 1, r2), (three_ref, 2, r3), (one_ref, 0, r1))

    def load(ref, i):
        slot = lax.rem(i, SLOTS)
        return pltpu.make_async_copy(
            ref.at[pl.ds(i * SUB, SUB)], buf.at[slot], load_sem.at[slot]
        )

    smalls = (
        pltpu.make_async_copy(start_hbm, start_ref, small_sem.at[0]),
        pltpu.make_async_copy(end_hbm, end_ref, small_sem.at[1]),
        pltpu.make_async_copy(table_hbm, table_ref, small_sem.at[2]),
    )
    load(sets[0][0], 0).start()
    for copy in smalls:
        copy.start()
    for i in range(1, SLOTS - 1):
        load(sets[0][0], i).start()
    for copy in smalls:
        copy.wait()

    scale_t = 1.0 / (samples ** 0.5)
    lane = lax.broadcasted_iota(jnp.int32, (receivers, LANES), 1).astype(f32)
    ticks = [(lane + c * LANES).astype(bf) for c in range(middle // LANES)]

    def column(row):
        row = jnp.broadcast_to(row.astype(f32), (LANES, receivers))
        return row.astype(bf).T

    def send(src, dst, sem, arrive, order):
        def one(p):
            pltpu.make_async_remote_copy(
                src_ref=src(p), dst_ref=dst, send_sem=sem, recv_sem=arrive,
                device_id={"freq": p}, device_id_type=pl.DeviceIdType.MESH,
            ).start()

        def far():
            @pl.loop(0, half)
            def _(q):
                one(peer_far(q))

        def near():
            pltpu.make_async_copy(src(me), dst, arrive).start()

            @pl.loop(1, half)
            def _(q):
                one(peer_near(q))

        far()
        near()

    for k, (ref, which, landing) in enumerate(sets):
        @pl.loop(0, chunks)
        def _(g):
            @pl.loop(0, CHUNK // SUB)
            def _(j):
                i = g * (CHUNK // SUB) + j
                ahead = i + SLOTS - 1

                @pl.when(ahead < total)
                def _():
                    load(ref, ahead).start()

                if k < 2:
                    @pl.when(ahead >= total)
                    def _():
                        load(sets[k + 1][0], ahead - total).start()

                load(ref, i).wait()
                slot = lax.rem(i, SLOTS)
                for s in range(SUB):
                    row = i * SUB + s
                    first = column(start_ref[which, pl.ds(row, 1), :])
                    last = column(end_ref[which, pl.ds(row, 1), :] - middle)
                    pieces = []
                    for c in range(samples // LANES):
                        x = buf[slot, s, :, c * LANES:(c + 1) * LANES]
                        tick = ticks[c % (middle // LANES)]
                        keep = tick >= first if c * LANES < middle else tick < last
                        pieces.append(jnp.where(keep, x, jnp.zeros_like(x)))
                    windowed = jnp.concatenate(pieces, axis=1)
                    spec = lax.dot_general(
                        table_ref[...], windowed, (((1,), (1,)), ((), ())),
                        preferred_element_type=f32,
                    )
                    at = pl.multiple_of((j * SUB + s) * waves, waves)
                    for c in range(receivers // LANES):
                        scr[c, pl.ds(at, waves), :] = spec[:, c * LANES:(c + 1) * LANES]

            for w in range(n):
                for c in range(receivers // LANES):
                    re = scr[c, pl.ds(2 * w, CHUNK, stride=waves), :]
                    im = scr[c, pl.ds(2 * w + 1, CHUNK, stride=waves), :]
                    both = jnp.concatenate([re, im], axis=0) * scale_t
                    stage[k, g, w, :, c * LANES:(c + 1) * LANES] = both.astype(bf)

            if k == 0:
                @pl.when(g == 0)
                def _():
                    pl.semaphore_wait(barrier, n - 1)

            arrive = r23_sem.at[k] if k < 2 else r1_sem.at[g]
            there = pl.ds(pl.multiple_of((g * n + me) * PAIR, PAIR), PAIR)
            send(lambda p: stage.at[k, g, p], landing.at[there], send_sem.at[k], arrive, 0)

    scale_f = 1.0 / (n ** 0.5)
    fold = math.frexp(scale_f)[0] == 0.5
    keep_rows = lax.broadcasted_iota(jnp.int32, (PAIR, samples), 0)
    for w in range(0, waves, 2):
        pair = table_ref[w:w + 2, :].astype(f32)
        if fold:
            pair = pair * scale_f
        spread = jnp.concatenate(
            [jnp.broadcast_to(pair[c:c + 1, :], (CHUNK, samples)) for c in range(2)], axis=0
        )
        for s in range(CHUNK):
            here = (keep_rows == s) | (keep_rows == s + CHUNK)
            wide_ref[s, w * CHUNK:(w + 2) * CHUNK, :] = jnp.where(
                here, spread, jnp.zeros_like(spread)
            ).astype(bf)

    drain(r3, r23_sem.at[1])

    @pl.loop(0, chunks * n)
    def _(b):
        rows = pl.ds(pl.multiple_of(b * PAIR, PAIR), PAIR)
        x = r3[rows, :].astype(f32)
        r3s[rows, :] = jnp.concatenate([x[CHUNK:], -x[:CHUNK]], axis=0).astype(bf)

    drain(r2, r23_sem.at[0])
    scale_g = 1.0 / ((n * sources) ** 0.5)
    scale_m = 1.0 / (receivers ** 0.5)
    width = 256
    dot = functools.partial(jnp.dot, preferred_element_type=f32)

    @pl.loop(0, receivers // width)
    def _(b):
        cols = pl.ds(pl.multiple_of(b * width, width), width)
        ct = r2[:, cols].T
        gw[cols, :receivers] = (dot(ct, r3[...]) * scale_g).astype(bf)
        gw[cols, receivers:] = (dot(ct, r3s[...]) * scale_g).astype(bf)

    span = n * PAIR

    @pl.loop(0, chunks)
    def _(g):
        rows = pl.ds(pl.multiple_of(g * span, span), span)
        drain(r1.at[rows], r1_sem.at[g])
        prod = dot(r1[rows, :], gw[...])
        for p in range(n):
            a = prod[p * PAIR:p * PAIR + CHUNK]
            b = prod[p * PAIR + CHUNK:(p + 1) * PAIR]
            re = a[:, :receivers] - b[:, receivers:]
            im = a[:, receivers:] + b[:, :receivers]
            mbuf[g, p] = (jnp.concatenate([re, im], axis=0) * scale_m).astype(bf)
        there = pl.ds(pl.multiple_of((g * n + me) * PAIR, PAIR), PAIR)
        send(lambda p: mbuf.at[g, p], piece.at[there], send_sem.at[3], out_sem.at[g], 1)

    @pl.loop(0, chunks - 1)
    def _(g):
        rows = pl.ds(pl.multiple_of(g * span, span), span)
        drain(piece.at[rows], out_sem.at[g])
        turned[...] = piece[rows, :].T

        @pl.loop(0, CHUNK)
        def _(s):
            early_ref[g * CHUNK + s] = inverse(turned[...], wide_ref[s], fold, scale_f)

    rows = pl.ds((chunks - 1) * span, span)
    drain(piece.at[rows], out_sem.at[chunks - 1])
    last_ref[...] = piece[rows, :].T
    for k in range(3):
        drain(stage.at[k, :, pl.ds(0, n - 1)], send_sem.at[k])
    drain(mbuf.at[:, pl.ds(0, n - 1)], send_sem.at[3])


def inverse(turned, wide, fold, scale):
    timed = jnp.dot(turned, wide, preferred_element_type=jnp.float32)
    if not fold:
        timed = timed * scale
    return timed.astype(jnp.bfloat16)


def write_kernel(n, early_ref, last_ref, wide_ref, out_ref, tail, early_sem, tail_sem):
    early = early_ref.shape[0]
    scale = 1.0 / (n ** 0.5)
    fold = math.frexp(scale)[0] == 0.5

    def bulk(g):
        at = pl.ds(g * CHUNK, CHUNK)
        return pltpu.make_async_copy(early_ref.at[at], out_ref.at[at], early_sem.at[g])

    for g in range(early // CHUNK):
        bulk(g).start()

    def rest(s):
        return pltpu.make_async_copy(tail.at[s], out_ref.at[early + s], tail_sem.at[s])

    @pl.loop(0, CHUNK)
    def _(s):
        tail[s] = inverse(last_ref[...], wide_ref[s], fold, scale)
        rest(s).start()

    for g in range(early // CHUNK):
        bulk(g).wait()

    @pl.loop(0, CHUNK)
    def _(s):
        rest(s).wait()


def spectrum(traces, start, finish, table, count):
    sources, receivers, samples = traces.shape
    times = jnp.arange(samples, dtype=jnp.int32)
    inside = (times >= start[:, :, None]) & (times < finish[:, :, None])
    windowed = jnp.where(inside, traces, jnp.zeros_like(traces))
    flat = windowed.reshape(sources * receivers, samples)
    spec = lax.dot_general(
        table, flat, (((1,), (1,)), ((), ())), preferred_element_type=jnp.float32
    )
    spec = spec * (1.0 / jnp.sqrt(jnp.float32(samples)))
    return spec.astype(jnp.bfloat16).reshape(count, 2, sources, receivers)


def correlate(first, second):
    swapped = jnp.stack([first[:, 1], -first[:, 0]], axis=1)
    left = jnp.stack([first, swapped], axis=1)
    cross = jnp.einsum("fkcsr,fcur->fksu", left, second, preferred_element_type=jnp.float32)
    cross = cross * (1.0 / jnp.sqrt(jnp.float32(first.shape[3])))
    return cross.astype(jnp.bfloat16)


def convolve(cross, third):
    right = jnp.stack(
        [
            jnp.stack([third[:, 0], -third[:, 1]], axis=1),
            jnp.stack([third[:, 1], third[:, 0]], axis=1),
        ],
        axis=1,
    )
    multiple = jnp.einsum("fcsu,fkcur->fksr", cross, right, preferred_element_type=jnp.float32)
    multiple = multiple * (1.0 / jnp.sqrt(jnp.float32(third.shape[2])))
    return multiple.astype(jnp.bfloat16)


def plain_on_device(primary_one, primary_two, primary_three, window_start, window_end):
    samples = primary_one.shape[2]
    count = F_DEV * lax.axis_size("freq")
    table = make_table(count, samples)
    spec_one = spectrum(primary_one, window_start[0], window_end[0], table, count)
    spec_two = spectrum(primary_two, window_start[1], window_end[1], table, count)
    spec_three = spectrum(primary_three, window_start[2], window_end[2], table, count)
    first, second, third = (
        lax.all_to_all(spec_one, "freq", split_axis=0, concat_axis=2, tiled=True),
        lax.all_to_all(spec_two, "freq", split_axis=0, concat_axis=2, tiled=True),
        lax.all_to_all(spec_three, "freq", split_axis=0, concat_axis=2, tiled=True),
    )
    cross = correlate(first, second)
    multiple = convolve(cross, third)
    piece = lax.all_to_all(multiple, "freq", split_axis=2, concat_axis=0, tiled=True)
    waves, parts, sources, receivers = piece.shape
    flat = piece.reshape(waves * parts, sources * receivers)
    timed = lax.dot_general(
        flat, table, (((0,), (0,)), ((), ())), preferred_element_type=jnp.float32
    )
    timed = timed * (1.0 / jnp.sqrt(jnp.float32(count)))
    return timed.astype(jnp.bfloat16).reshape(sources, receivers, samples)


def on_device(primary_one, primary_two, primary_three, window_start, window_end):
    sources, receivers, samples = primary_one.shape
    n = lax.axis_size("freq")
    fits = sources * receivers * samples * 2 <= 16 << 20 and n * sources <= 512 and samples <= 512
    if not fits or n > 16 or n % 2 or sources % CHUNK or receivers % 256 or samples % (2 * LANES):
        return plain_on_device(
            primary_one, primary_two, primary_three, window_start, window_end
        )
    table = host_table(F_DEV * n, samples)
    bf = jnp.bfloat16
    chunks = sources // CHUNK
    rows = chunks * n * PAIR
    span = n * PAIR
    vmem = pl.BlockSpec(memory_space=pltpu.VMEM)
    hbm = pl.BlockSpec(memory_space=pl.ANY)
    early, last, wide = pl.pallas_call(
        functools.partial(exchange_kernel, n),
        out_shape=(
            pltpu.VMEM((sources - CHUNK, receivers, samples), bf),
            pltpu.VMEM((receivers, span), bf),
            pltpu.VMEM((CHUNK, span, samples), bf),
        ),
        in_specs=[hbm] * 6,
        out_specs=(vmem, vmem, vmem),
        scratch_shapes=[
            pltpu.VMEM(window_start.shape, jnp.int32),
            pltpu.VMEM(window_end.shape, jnp.int32),
            pltpu.VMEM(table.shape, bf),
            pltpu.VMEM((SLOTS, SUB, receivers, samples), bf),
            pltpu.VMEM((receivers // LANES, CHUNK * 2 * n, LANES), jnp.float32),
            pltpu.VMEM((3, chunks, n, PAIR, receivers), bf),
            pltpu.VMEM((rows, receivers), bf),
            pltpu.VMEM((rows, receivers), bf),
            pltpu.VMEM((rows, receivers), bf),
            pltpu.VMEM((rows, receivers), bf),
            pltpu.VMEM((receivers, 2 * receivers), bf),
            pltpu.VMEM((chunks, n, PAIR, receivers), bf),
            pltpu.VMEM((rows, receivers), bf),
            pltpu.VMEM((receivers, span), bf),
            pltpu.SemaphoreType.DMA((SLOTS,)),
            pltpu.SemaphoreType.DMA((3,)),
            pltpu.SemaphoreType.DMA((4,)),
            pltpu.SemaphoreType.DMA((chunks,)),
            pltpu.SemaphoreType.DMA((2,)),
            pltpu.SemaphoreType.DMA((chunks,)),
        ],
        compiler_params=pltpu.CompilerParams(
            collective_id=0, has_side_effects=True, vmem_limit_bytes=40 << 20,
        ),
        name="exchange",
    )(primary_one, primary_two, primary_three, window_start, window_end, table)
    return pl.pallas_call(
        functools.partial(write_kernel, n),
        out_shape=jax.ShapeDtypeStruct(primary_one.shape, bf),
        in_specs=[vmem, vmem, vmem],
        out_specs=hbm,
        scratch_shapes=[
            pltpu.VMEM((CHUNK, receivers, samples), bf),
            pltpu.SemaphoreType.DMA((chunks,)),
            pltpu.SemaphoreType.DMA((CHUNK,)),
        ],
        compiler_params=pltpu.CompilerParams(vmem_limit_bytes=20 << 20),
        name="write",
    )(early, last, wide)


def solution(mesh):
    return jax.shard_map(
        on_device,
        mesh=mesh,
        in_specs=(
            P(("groups", "freq"), None, None),
            P(("groups", "freq"), None, None),
            P(("groups", "freq"), None, None),
            P(None, ("groups", "freq"), None),
            P(None, ("groups", "freq"), None),
        ),
        out_specs=P(("groups", "freq"), None, None),
        check_vma=False,
    )
```

time: 117 us -> 106 us (0.906)
  Pallas kernels: 115 us -> 106 us
    pallas_call x2, Pallas kernels: 115 us -> 106 us  [the longest x1 99.8 us: on_device(): pl.pallas_call(functools.partial(exchange_kernel, n), out_shape=(pltpu.VM...]
where the time goes in v1:
time: 106 us
  Pallas kernels  106 us (100%)
    pallas_call x1, Pallas kernels, on_device(): pl.pallas_call(functools.partial(exchange_kernel, n), out_shape=(pltpu.VM...  99.8 us
    pallas_call x1, Pallas kernels, on_device(): pl.pallas_call(functools.partial(write_kernel, n), out_shape=jax.ShapeDty...  5.91 us

profile of v1, /device:TPU:1, one launch (start us, length us, event | category | flops | bytes accessed | tf_op | source)
XLA Modules:
  0.0 105.7 jit_solution(2417037720063204864)
XLA Ops:
  0.0 99.8 %exchange.1 = (bf16[24,512,512]{2,1,0:T(8,128)(2,1)S(1)}, bf16[512,256]{1,0:T(8,128)(2,1)S(1)}, bf16[8,256,512]{2,1,0:T(8,128)(2,1)S(1)}) custom-call(bf16[32,512,512]{2,1,0:T(8,128)(2,1)} %one_ref.1, bf16[32,512,512]{2,1,0:T(8,128)(2,1)} %two_ref.1, bf16[32,512,512]{2,1,0:T(8,128)(2,1)} %three_ref.1, s32[3,32,512]{2,1,0:T(8,128)} %start_hbm.1, ...), custom_call_target="tpu_custom_call" | custom-call | tf_op jit(solution)/shard_map/exchange/pallas_call | solution.py:358
  99.8 5.9 %write.1 = bf16[32,512,512]{2,1,0:T(8,128)(2,1)} custom-call(bf16[24,512,512]{2,1,0:T(8,128)(2,1)S(1)} %get-tuple-element.8.early_ref, bf16[512,256]{1,0:T(8,128)(2,1)S(1)} %get-tuple-element.9.last_ref, bf16[8,256,512]{2,1,0:T(8,128)(2,1)S(1)} %get-tuple-element.10.wide_ref), custom_call_target="tpu_custom_call" | custom-call | tf_op jit(solution)/shard_map/write/pallas_call | solution.py:394
